TPU v7x, 32 devices: a whole 2x2x4 slice. The times are simulated.
32 devices in a mesh: dp: 8 (over z, y), head: 4 (over x, core).
Axes of the slice: x: 2, y: 2, z: 4, core: 2. Of those that a mesh axis runs over, the one named last changes fastest.
Arguments:
- tokens: bfloat16 [32768, 768], P(('dp', 'head')), may hold values from -6 to 6
- seq_lengths: int32 [64, 32], P('dp'), may hold values from 0 to 512, as said below
- qkv_weight: bfloat16 [2, 3, 768, 768], P(None, None, None, 'head'), may hold values from -0.21875 to 0.21875
- qv_bias: float32 [2, 2, 768], P(None, None, 'head'), may hold values from -3 to 3
- out_weight: bfloat16 [2, 768, 768], replicated, may hold values from -0.875 to 0.875
- out_bias: float32 [2, 768], replicated, may hold values from -3 to 3
- norm1_gain: float32 [2, 768], replicated, may hold values from 0.25 to 1.75
- norm1_shift: float32 [2, 768], replicated, may hold values from -3 to 3
- up_weight: bfloat16 [2, 768, 3072], replicated, may hold values from -0.21875 to 0.21875
- up_bias: float32 [2, 3072], replicated, may hold values from -3 to 3
- down_weight: bfloat16 [2, 3072, 768], replicated, may hold values from -0.109375 to 0.109375
- down_bias: float32 [2, 768], replicated, may hold values from -3 to 3
- norm2_gain: float32 [2, 768], replicated, may hold values from 0.25 to 1.75
- norm2_shift: float32 [2, 768], replicated, may hold values from -3 to 3
- out_grad: bfloat16 [32768, 768], P(('dp', 'head')), may hold values from -6 to 6
Outputs:
- out_state: bfloat16 [32768, 768], P(('dp', 'head'))
- input_grad: bfloat16 [32768, 768], P(('dp', 'head'))
- qkv_weight_grad: float32 [2, 3, 768, 768], P(None, None, 'dp', 'head')
- qv_bias_grad: float32 [2, 2, 768], replicated
- out_weight_grad: float32 [2, 768, 768], P(None, 'dp', 'head')
- out_bias_grad: float32 [2, 768], replicated
- norm1_gain_grad: float32 [2, 768], replicated
- norm1_shift_grad: float32 [2, 768], replicated
- up_weight_grad: float32 [2, 768, 3072], P(None, 'dp', 'head')
- up_bias_grad: float32 [2, 3072], replicated
- down_weight_grad: float32 [2, 3072, 768], P(None, 'head', 'dp')
- down_bias_grad: float32 [2, 768], replicated
- norm2_gain_grad: float32 [2, 768], replicated
- norm2_shift_grad: float32 [2, 768], replicated
Inputs may be any that keep to these rules, and one draw needn't show every extreme that they name: `seq_lengths`: each slot's row sums to 512; nonzero entries come first and zero entries mark no sequence; some slot holds a single sequence of 512 rows.
All inputs are finite; a program needn't handle non-finite values.
Results may differ from a plain program's by a relative error of at most 0.025.
Values may be sent and summed in bfloat16 or wider, within the bound.
No kernel may reach another device: no remote copies, remote signals or barrier semaphores. Data moves between devices by JAX's collectives and lax.ppermute only.
A program may use at most 256 MiB of HBM per device.

v0:
```python
import jax
import jax.numpy as jnp
from jax import lax
from jax.sharding import PartitionSpec as P

HD = 64
EPSILON = 1e-06


def norm_rows(values, gain, shift):
    centre = jnp.mean(values, axis=-1, keepdims=True)
    centred = values - centre
    spread = jnp.mean(centred * centred, axis=-1, keepdims=True)
    return centred * lax.rsqrt(spread + EPSILON) * gain + shift


def exact_gelu(values):
    return jax.nn.gelu(values, approximate=False)


def segment_ids(lengths, slot_rows):
    boundary = jnp.cumsum(lengths, axis=1)
    position = jnp.arange(slot_rows, dtype=jnp.int32)
    return jnp.sum((position[None, :, None] >= boundary[:, None, :]).astype(jnp.int32), axis=2)


def slot_scores(queries, keys_in, segments):
    scaling = queries.shape[-1] ** (-0.5)
    scores = (
        jnp.einsum("qhd,khd->hqk", queries, keys_in, preferred_element_type=jnp.float32) * scaling
    )
    inside = (segments[:, None] == segments[None, :])[None]
    return (scores, inside)


def slot_forward(packed):
    queries, keys_in, values_in, segments = packed
    scores, inside = slot_scores(queries, keys_in, segments)
    scores = jnp.where(inside, scores, -1e30)
    peak_score = jnp.max(scores, axis=-1, keepdims=True)
    weights = jnp.exp(scores - peak_score)
    denominator = jnp.sum(weights, axis=-1, keepdims=True)
    probability = (weights / denominator).astype(jnp.bfloat16)
    context = jnp.einsum("hqk,khd->qhd", probability, values_in, preferred_element_type=jnp.float32)
    return (context.astype(jnp.bfloat16), (peak_score + jnp.log(denominator))[..., 0])


def slot_backward(packed):
    queries, keys_in, values_in, grad_context, log_total, segments = packed
    scaling = queries.shape[-1] ** (-0.5)
    scores, inside = slot_scores(queries, keys_in, segments)
    probability = jnp.where(inside, jnp.exp(scores - log_total[..., None]), 0.0)
    grad_prob = jnp.einsum(
        "qhd,khd->hqk", grad_context, values_in, preferred_element_type=jnp.float32
    )
    shares = jnp.sum(probability * grad_prob, axis=-1, keepdims=True)
    grad_score = (probability * (grad_prob - shares)).astype(jnp.bfloat16)
    grad_query = (
        jnp.einsum("hqk,khd->qhd", grad_score, keys_in, preferred_element_type=jnp.float32)
        * scaling
    )
    grad_key = (
        jnp.einsum("hqk,qhd->khd", grad_score, queries, preferred_element_type=jnp.float32)
        * scaling
    )
    grad_value = jnp.einsum(
        "hqk,qhd->khd",
        probability.astype(jnp.bfloat16),
        grad_context,
        preferred_element_type=jnp.float32,
    )
    return (
        grad_query.astype(jnp.bfloat16),
        grad_key.astype(jnp.bfloat16),
        grad_value.astype(jnp.bfloat16),
    )


def on_device(
    tokens,
    seq_lengths,
    qkv_weight,
    qv_bias,
    out_weight,
    out_bias,
    norm1_gain,
    norm1_shift,
    up_weight,
    up_bias,
    down_weight,
    down_bias,
    norm2_gain,
    norm2_shift,
    out_grad,
):
    heads_count = lax.axis_size("head")
    head_index = lax.axis_index("head")
    local_rows, model_width = tokens.shape
    group_rows = local_rows * heads_count
    slots_here = seq_lengths.shape[0]
    slot_rows = group_rows // slots_here
    segments = segment_ids(seq_lengths, slot_rows)
    head_width = qkv_weight.shape[-1]
    local_heads = head_width // HD
    layers = qkv_weight.shape[0]
    qkv_shape = (slots_here, slot_rows, 3, local_heads, HD)
    hidden_state = tokens.astype(jnp.float32)
    kept_values = []
    for layer_index in range(layers):
        gathered = lax.all_gather(hidden_state.astype(jnp.bfloat16), "head", axis=0, tiled=True)
        projected = jnp.einsum(
            "rd,cde->rce", gathered, qkv_weight[layer_index], preferred_element_type=jnp.float32
        )
        bias_rows = jnp.stack(
            [
                qv_bias[layer_index, 0],
                jnp.zeros_like(qv_bias[layer_index, 0]),
                qv_bias[layer_index, 1],
            ]
        )
        projected = (projected + bias_rows[None]).astype(jnp.bfloat16)
        shaped = projected.reshape(qkv_shape)
        context, log_total = lax.map(
            slot_forward, (shaped[:, :, 0], shaped[:, :, 1], shaped[:, :, 2], segments)
        )
        context = context.reshape(group_rows, head_width)
        token_context = lax.all_to_all(context, "head", split_axis=0, concat_axis=1, tiled=True)
        attended = (
            jnp.dot(token_context, out_weight[layer_index], preferred_element_type=jnp.float32)
            + out_bias[layer_index]
        )
        first_sum = hidden_state + attended
        normed = norm_rows(first_sum, norm1_gain[layer_index], norm1_shift[layer_index])
        normed_low = normed.astype(jnp.bfloat16)
        ffn_rows = normed_low
        up_part = up_weight[layer_index]
        up_shift = up_bias[layer_index]
        down_part = down_weight[layer_index]
        before_gelu = jnp.dot(ffn_rows, up_part, preferred_element_type=jnp.float32) + up_shift
        activated = exact_gelu(before_gelu).astype(jnp.bfloat16)
        branch = jnp.dot(activated, down_part, preferred_element_type=jnp.float32)
        second_sum = normed + branch + down_bias[layer_index]
        hidden_state = norm_rows(second_sum, norm2_gain[layer_index], norm2_shift[layer_index])
        kept_values.append(
            (
                gathered,
                projected,
                log_total,
                token_context,
                first_sum,
                ffn_rows,
                up_part,
                down_part,
                before_gelu,
                activated,
                second_sum,
            )
        )
    out_state = hidden_state.astype(jnp.bfloat16)
    grad_state = out_grad.astype(jnp.float32)
    ffn_list, proj_list, attn_list, small_list, shift_list = ([], [], [], [], [])
    for layer_index in reversed(range(layers)):
        (
            gathered,
            projected,
            log_total,
            token_context,
            first_sum,
            ffn_rows,
            up_part,
            down_part,
            before_gelu,
            activated,
            second_sum,
        ) = kept_values[layer_index]
        pull_second = jax.vjp(
            norm_rows, second_sum, norm2_gain[layer_index], norm2_shift[layer_index]
        )[1]
        grad_second, grad_gain2, grad_shift2 = pull_second(grad_state)
        grad_branch = grad_second.astype(jnp.bfloat16)
        grad_down_shift = jnp.sum(grad_branch.astype(jnp.float32), axis=0)
        grad_down = jnp.einsum(
            "rd,rf->df", grad_branch, activated, preferred_element_type=jnp.float32
        )
        grad_act = jnp.einsum(
            "rd,fd->rf", grad_branch, down_part, preferred_element_type=jnp.float32
        )
        pull_gelu = jax.vjp(exact_gelu, before_gelu)[1]
        grad_pre = pull_gelu(grad_act)[0].astype(jnp.bfloat16)
        grad_up_shift = jnp.sum(grad_pre.astype(jnp.float32), axis=0)
        grad_up = jnp.einsum("rd,rf->df", ffn_rows, grad_pre, preferred_element_type=jnp.float32)
        grad_normed_low = jnp.einsum(
            "rf,df->rd", grad_pre, up_part, preferred_element_type=jnp.float32
        )
        grad_normed = grad_second + grad_normed_low
        pull_first = jax.vjp(
            norm_rows, first_sum, norm1_gain[layer_index], norm1_shift[layer_index]
        )[1]
        grad_first, grad_gain1, grad_shift1 = pull_first(grad_normed)
        grad_attended = grad_first.astype(jnp.bfloat16)
        grad_out_shift = jnp.sum(grad_attended.astype(jnp.float32), axis=0)
        grad_out = jnp.einsum(
            "rd,re->de", token_context, grad_attended, preferred_element_type=jnp.float32
        )
        grad_mixed = jnp.einsum(
            "re,de->rd", grad_attended, out_weight[layer_index], preferred_element_type=jnp.float32
        ).astype(jnp.bfloat16)
        grad_context = lax.all_to_all(grad_mixed, "head", split_axis=1, concat_axis=0, tiled=True)
        shaped = projected.reshape(qkv_shape)
        grad_query, grad_key, grad_value = lax.map(
            slot_backward,
            (
                shaped[:, :, 0],
                shaped[:, :, 1],
                shaped[:, :, 2],
                grad_context.reshape(slots_here, slot_rows, local_heads, HD),
                log_total,
                segments,
            ),
        )
        grad_proj = jnp.stack([grad_query, grad_key, grad_value], axis=2).reshape(
            group_rows, 3, head_width
        )
        grad_qkv = jnp.einsum(
            "rd,rce->cde", gathered, grad_proj, preferred_element_type=jnp.float32
        )
        bias_local = jnp.sum(grad_proj.astype(jnp.float32), axis=0)
        qv_local = jnp.stack([bias_local[0], bias_local[2]])
        qv_full = lax.dynamic_update_slice_in_dim(
            jnp.zeros((2, model_width), jnp.float32), qv_local, head_index * head_width, 1
        )
        layer_weights = qkv_weight[layer_index]
        grad_state = grad_first + lax.psum_scatter(
            jnp.einsum(
                "rce,cde->rd", grad_proj, layer_weights, preferred_element_type=jnp.float32
            ).astype(jnp.bfloat16),
            "head",
            scatter_dimension=0,
            tiled=True,
        ).astype(jnp.float32)
        ffn_list.append(jnp.stack([grad_up, grad_down]))
        proj_list.append(grad_out)
        attn_list.append(grad_qkv)
        small_list.append(
            jnp.concatenate(
                [
                    qv_full,
                    jnp.stack(
                        [
                            grad_out_shift,
                            grad_gain1,
                            grad_shift1,
                            grad_down_shift,
                            grad_gain2,
                            grad_shift2,
                        ]
                    ),
                ],
                axis=0,
            )
        )
        shift_list.append(grad_up_shift)
    input_grad = grad_state.astype(jnp.bfloat16)
    ffn_stack = jnp.stack(ffn_list[::-1])
    proj_stack = jnp.stack(proj_list[::-1])
    attn_stack = jnp.stack(attn_list[::-1])
    small_stack = jnp.stack(small_list[::-1])
    shift_stack = jnp.stack(shift_list[::-1])
    ffn_data, proj_data, attn_data = (
        lax.psum_scatter(
            ffn_stack.astype(jnp.bfloat16), "dp", scatter_dimension=2, tiled=True
        ).astype(jnp.float32),
        lax.psum_scatter(
            proj_stack.astype(jnp.bfloat16), "dp", scatter_dimension=1, tiled=True
        ).astype(jnp.float32),
        lax.psum_scatter(
            attn_stack.astype(jnp.bfloat16), "dp", scatter_dimension=2, tiled=True
        ).astype(jnp.float32),
    )
    ffn_head, proj_head = (
        lax.psum_scatter(
            ffn_data.astype(jnp.bfloat16), "head", scatter_dimension=3, tiled=True
        ).astype(jnp.float32),
        lax.psum_scatter(
            proj_data.astype(jnp.bfloat16), "head", scatter_dimension=2, tiled=True
        ).astype(jnp.float32),
    )
    small_sum, shift_sum = lax.psum((small_stack, shift_stack), ("dp", "head"))
    down_weight_grad = jnp.transpose(ffn_head[:, 1], (0, 2, 1))
    return (
        out_state,
        input_grad,
        attn_data,
        small_sum[:, 0:2],
        proj_head,
        small_sum[:, 2],
        small_sum[:, 3],
        small_sum[:, 4],
        ffn_head[:, 0],
        shift_sum,
        down_weight_grad,
        small_sum[:, 5],
        small_sum[:, 6],
        small_sum[:, 7],
    )


def solution(mesh):
    in_specs = (
        P(("dp", "head"), None),
        P("dp", None),
        P(None, None, None, "head"),
        P(None, None, "head"),
        P(),
        P(),
        P(),
        P(),
        P(),
        P(),
        P(),
        P(),
        P(),
        P(),
        P(("dp", "head"), None),
    )
    out_specs = (
        P(("dp", "head"), None),
        P(("dp", "head"), None),
        P(None, None, "dp", "head"),
        P(),
        P(None, "dp", "head"),
        P(),
        P(),
        P(),
        P(None, "dp", "head"),
        P(),
        P(None, "head", "dp"),
        P(),
        P(),
        P(),
    )
    return jax.shard_map(
        on_device, mesh=mesh, in_specs=in_specs, out_specs=out_specs, check_vma=False
    )
```

profile of v0, /device:TPU:0, one launch (start us, length us, event | category | flops | bytes accessed | tf_op | source)
XLA Modules:
  0.0 1406.1 jit_solution(3311266776964060774)
XLA Ops:
  12.9 45.8 %all-gather.3.cloned.1.call-done = bf16[4096,768]{1,0:T(8,128)(2,1)} async-done(((bf16[1024,768]{1,0:T(8,128)(2,1)}), bf16[4096,768]{1,0:T(8,128)(2,1)}) %all-gather.3.cloned.1.call-update) | async-done | bytes 6291472 | tf_op jit(solution)/shard_map/all_gather | solution.py:110
  73.9 35.4 %while.52 = (s32[]{:T(128)}, bf16[8,512,3,64]{1,3,2,0:T(8,128)(2,1)}, f32[8,3,512]{2,1,0:T(4,128)S(1)}, bf16[8,512,3,64]{1,3,2,0:T(8,128)(2,1)}, s32[8,512]{1,0:...) while((s32[]{:T(128)}, ...), condition=%wide.region_5.6_spmd, body=%wide.region_2.5_spmd.sunk | while | flops 211122688 | bytes 11335773 | solution.py:123
  113.8 13.7 all_to_all.52
  139.1 15.2 %all-to-all-done = bf16[4,1024,192]{1,2,0:T(8,128)(2,1)S(1)} async-done(((bf16[4,1024,192]{1,2,0:T(8,128)(2,1)}), bf16[4,1024,192]{1,2,0:T(8,128)(2,1)S(1)}, u32[]{:S(2)}, u32[]{:S(2)}) %all-to-all-start) | async-done | bytes 1572896 | tf_op jit(solution)/shard_map/all_to_all | solution.py:127
  158.9 38.8 %multiply_convert_fusion.3 = (bf16[1024,3072]{1,0:T(8,128)(2,1)}, f32[1024,3072]{1,0:T(8,128)}, f32[1024,3072]{1,0:T(8,128)}) fusion(f32[3072]{0:T(1024)S(1)} %bitcast.494, bf16[2,768,3072]{2,1,0:T(8,128)(2,1)} %param.31, f32[1024,768]{0,1:T(8,128)S(1)} %get-tuple-element.478, f32[768]{0:T(1024)S(1)} %get-tuple-element.347, ...), kind=kOutput, calls=%fused_computation.148 | convolution fusion | flops 5043388416 | bytes 39348224 | tf_op jit(solution)/shard_map/dot_general | solution.py:139
  208.6 46.5 %all-gather.5.cloned.1.call-done = bf16[4096,768]{0,1:T(8,128)(2,1)} async-done(((bf16[1024,768]{0,1:T(8,128)(2,1)}), bf16[4096,768]{0,1:T(8,128)(2,1)}) %all-gather.5.cloned.1.call-update) | async-done | bytes 6291472 | tf_op jit(solution)/shard_map/all_gather | solution.py:110
  273.1 43.5 %while.53 = (s32[]{:T(128)}, bf16[8,512,3,64]{1,3,2,0:T(8,128)(2,1)}, f32[8,3,512]{2,1,0:T(4,128)S(1)}, bf16[8,512,3,64]{1,3,2,0:T(8,128)(2,1)}, s32[8,512]{1,0:...) while((s32[]{:T(128)}, ...), condition=%wide.region_13.14_spmd, body=%wide.region_10.13_spmd.sunk | while | flops 211122688 | bytes 11335773 | solution.py:123
  334.3 17.5 %all-to-all-done.1 = bf16[4,1024,192]{1,2,0:T(8,128)(2,1)} async-done(((bf16[4,1024,192]{1,2,0:T(8,128)(2,1)}), bf16[4,1024,192]{1,2,0:T(8,128)(2,1)}, u32[]{:S(2)}, u32[]{:S(2)}) %all-to-all-start.1) | async-done | bytes 1572896 | tf_op jit(solution)/shard_map/all_to_all | solution.py:127
  356.5 38.4 %multiply_convert_fusion.2 = (bf16[1024,3072]{1,0:T(8,128)(2,1)}, f32[1024,3072]{1,0:T(8,128)}, f32[1024,3072]{1,0:T(8,128)}) fusion(f32[3072]{0:T(1024)S(1)} %bitcast.497, bf16[2,768,3072]{2,1,0:T(8,128)(2,1)} %param.31, f32[1024,768]{0,1:T(8,128)S(1)} %get-tuple-element.483, f32[768]{0:T(1024)S(1)} %copy-done.73, f32[768]{0:T(1024)S(1)} %copy-done.52, ...), kind=kOutput, calls=%fused_computation.135 | convolution fusion | flops 5043388416 | bytes 39348224 | tf_op jit(solution)/shard_map/dot_general | solution.py:139
  411.1 18.2 %convert_reduce_fusion = (f32[3072]{0:T(1024)}, bf16[1024,3072]{1,0:T(8,128)(2,1)}) fusion(f32[1024,3072]{1,0:T(8,128)} %get-tuple-element.435, bf16[1024,768]{0,1:T(8,128)(2,1)S(1)} %get-tuple-element.425, bf16[2,3072,768]{2,1,0:T(8,128)(2,1)} %param.33, f32[1024,3072]{1,0:T(8,128)} %get-tuple-element.484, f32[3072]{0:T(1024)S(1)} %bitcast.498), kind=kOutput, calls=%fused_computation.131 | convolution fusion | flops 4885312512 | bytes 37773312 | tf_op jit(solution)/shard_map/rd,fd->rf/dot_general | solution.py:185
  429.4 11.7 multiply_reduce_fusion.2
  451.5 20.0 %all-to-all-done.2 = bf16[1024,4,192]{0,2,1:T(8,128)(2,1)S(1)} async-done(((bf16[1024,4,192]{0,2,1:T(8,128)(2,1)}), bf16[1024,4,192]{0,2,1:T(8,128)(2,1)S(1)}, u32[]{:S(2)}, u32[]{:S(2)}) %all-to-all-start.2) | async-done | bytes 1572896 | tf_op jit(solution)/shard_map/all_to_all | solution.py:208
  479.6 88.1 %while.54 = (s32[]{:T(128)}, bf16[8,512,3,64]{1,3,2,0:T(8,128)(2,1)S(1)}, bf16[8,512,3,64]{1,3,2,0:T(8,128)(2,1)}, bf16[8,512,3,64]{1,3,2,0:T(8,128)(2,1)}, bf16...) while((s32[]{:T(128)}, ...), condition=%wide.region_24.25_spmd, body=%wide.region_22.24_spmd.sunk | while | flops 511146496 | bytes 26125428 | solution.py:210
  598.8 11.7 fusion.140
  610.5 41.4 %reduce-scatter.12.cloned.1.call-done = bf16[1024,768]{0,1:T(8,128)(2,1)} async-done(((bf16[4096,768]{0,1:T(8,128)(2,1)}), bf16[1024,768]{0,1:T(8,128)(2,1)}) %reduce-scatter.12.cloned.1.call-update) | async-done | bytes 1572880 | tf_op jit(solution)/shard_map/reduce_scatter | solution.py:233
  659.1 18.5 %convert_reduce_fusion.1 = (f32[3072]{0:T(1024)S(1)}, bf16[1024,3072]{1,0:T(8,128)(2,1)}) fusion(f32[1024,3072]{1,0:T(8,128)} %get-tuple-element.437, bf16[1024,768]{0,1:T(8,128)(2,1)} %get-tuple-element.421, bf16[2,3072,768]{2,1,0:T(8,128)(2,1)} %param.33, f32[1024,3072]{1,0:T(8,128)} %get-tuple-element.479, f32[3072]{0:T(1024)S(1)} %bitcast.495), kind=kOutput, calls=%fused_computation.132 | convolution fusion | flops 4885312512 | bytes 37773312 | tf_op jit(solution)/shard_map/rd,fd->rf/dot_general | solution.py:185
  738.1 16.7 %pad_maximum_fusion = bf16[2,2,768,3072]{3,2,1,0:T(8,128)(2,1)} fusion(bf16[1,2,768,3072]{3,2,1,0:T(8,128)(2,1)} %maximum_bitcast_fusion.1, bf16[1,2,768,3072]{3,2,1,0:T(8,128)(2,1)} %maximum_bitcast_fusion), kind=kLoop, calls=%fused_computation.126 | loop fusion | flops 9437184 | bytes 37748736 | tf_op jit(solution)/shard_map/stack | solution.py:264
  802.2 101.9 %while.55 = (s32[]{:T(128)}, bf16[8,512,3,64]{1,3,2,0:T(8,128)(2,1)}, bf16[8,512,3,64]{1,3,2,0:T(8,128)(2,1)}, bf16[8,512,3,64]{1,3,2,0:T(8,128)(2,1)}, bf16[8,5...) while((s32[]{:T(128)}, ...), condition=%wide.region_32.33_spmd, body=%wide.region_30.32_spmd.sunk | while | flops 511146496 | bytes 26125428 | solution.py:210
  966.8 112.1 %reduce-scatter.18.cloned.1.call-done = bf16[2,2,96,3072]{3,2,1,0:T(8,128)(2,1)} async-done(((bf16[2,2,768,3072]{3,2,1,0:T(8,128)(2,1)}), bf16[2,2,96,3072]{3,2,1,0:T(8,128)(2,1)}) %reduce-scatter.18.cloned.1.call-update) | async-done | bytes 2359312 | tf_op jit(solution)/shard_map/reduce_scatter | solution.py:270
  1081.6 122.8 %all-reduce.3.cloned.1.call-done = (f32[2,8,768]{2,0,1:T(2,128)}, f32[2,3072]{1,0:T(2,128)}) async-done(((f32[2,8,768]{2,0,1:T(2,128)}, f32[2,3072]{1,0:T(2,128)}), (f32[2,8,768]{2,0,1:T(2,128)}, f32[2,3072]{1,0:T(2,128)})) %all-reduce.3.cloned.1.call-update) | async-done | bytes 73744 | tf_op jit(solution)/shard_map/psum | solution.py:288
  1207.1 69.8 %reduce-scatter.22.cloned.1.call-done = bf16[96,1152]{1,0:T(8,128)(2,1)} async-done(((bf16[768,1152]{1,0:T(8,128)(2,1)}), bf16[96,1152]{1,0:T(8,128)(2,1)}) %reduce-scatter.22.cloned.1.call-update) | async-done | bytes 221200
  1281.1 18.6 %reduce-scatter.24.cloned.1.call-done = bf16[192,192]{1,0:T(8,128)(2,1)} async-done(((bf16[768,192]{1,0:T(8,128)(2,1)}), bf16[192,192]{1,0:T(8,128)(2,1)}) %reduce-scatter.24.cloned.1.call-update) | async-done | bytes 73744
  1301.4 59.1 %reduce-scatter.14.cloned.1.call-done = bf16[1024,768]{0,1:T(8,128)(2,1)} async-done(((bf16[4096,768]{0,1:T(8,128)(2,1)}), bf16[1024,768]{0,1:T(8,128)(2,1)}) %reduce-scatter.14.cloned.1.call-update) | async-done | bytes 1572880 | tf_op jit(solution)/shard_map/reduce_scatter | solution.py:233
  1366.3 29.9 %reduce-scatter.20.cloned.1.call-done = bf16[2,2,96,768]{3,2,1,0:T(8,128)(2,1)} async-done(((bf16[2,2,96,3072]{3,2,1,0:T(8,128)(2,1)}), bf16[2,2,96,768]{3,2,1,0:T(8,128)(2,1)}) %reduce-scatter.20.cloned.1.call-update) | async-done | bytes 589840 | tf_op jit(solution)/shard_map/reduce_scatter | solution.py:281
  (599 shorter events, 623.1 us)
Async XLA Ops:
  7.2 51.5 %all-gather.3.cloned.1.call-start = ((), (), s32[]{:S(2)}) async-start(), calls=%async_computation.11 | async-start | bytes 7864320 | tf_op jit(solution)/shard_map/all_gather | solution.py:110
  130.6 23.8 %all-to-all-start = ((bf16[4,1024,192]{1,2,0:T(8,128)(2,1)}), bf16[4,1024,192]{1,2,0:T(8,128)(2,1)S(1)}, u32[]{:S(2)}, u32[]{:S(2)}) async-start(bf16[4,1024,192]{1,2,0:T(8,128)(2,1)} %copy.160), calls=%async_computation | async-start | bytes 3145728 | tf_op jit(solution)/shard_map/all_to_all | solution.py:127
  134.3 120.8 %all-gather.5.cloned.1.call-start = ((), (), s32[]{:S(2)}) async-start(), calls=%async_computation.12 | async-start | bytes 7864320 | tf_op jit(solution)/shard_map/all_gather | solution.py:110
  137.9 59.8 %copy-start.50 = (f32[768]{0:T(1024)}, f32[768]{0:T(1024)S(1)}, u32[]{:S(2)}) copy-start(f32[768]{0:T(1024)S(1)} %get-tuple-element.495) | copy-start | bytes 9220
  137.9 59.8 %copy-start.71 = (f32[768]{0:T(1024)}, f32[768]{0:T(1024)S(1)}, u32[]{:S(2)}) copy-start(f32[768]{0:T(1024)S(1)} %get-tuple-element.347) | copy-start | bytes 9220
  138.5 213.3 %copy-start.35 = (f32[768]{0:T(1024)}, f32[768]{0:T(1024)S(1)}, u32[]{:S(2)}) copy-start(f32[768]{0:T(1024)S(1)} %get-tuple-element.497) | copy-start | bytes 9220
  206.4 145.4 %copy-start = (f32[1024,768]{0,1:T(8,128)}, f32[1024,768]{0,1:T(8,128)S(1)}, u32[]{:S(2)}) copy-start(f32[1024,768]{0,1:T(8,128)S(1)} %get-tuple-element.481) | copy-start | bytes 9437188
  206.4 145.4 %copy-start.33 = (f32[1024]{0:T(1024)}, f32[1024]{0:T(1024)S(1)}, u32[]{:S(2)}) copy-start(f32[1024]{0:T(1024)S(1)} %broadcast_multiply_fusion.2) | copy-start | bytes 12292
  206.8 145.0 %copy-start.37 = (f32[1024]{0:T(1024)}, f32[1024]{0:T(1024)S(1)}, u32[]{:S(2)}) copy-start(f32[1024]{0:T(1024)S(1)} %fusion.190) | copy-start | bytes 12292
  327.0 24.8 %all-to-all-start.1 = ((bf16[4,1024,192]{1,2,0:T(8,128)(2,1)}), bf16[4,1024,192]{1,2,0:T(8,128)(2,1)}, u32[]{:S(2)}, u32[]{:S(2)}) async-start(bf16[4,1024,192]{1,2,0:T(8,128)(2,1)} %copy.166), calls=%async_computation.1 | async-start | bytes 3145728 | tf_op jit(solution)/shard_map/all_to_all | solution.py:127
  447.9 23.6 %all-to-all-start.2 = ((bf16[1024,4,192]{0,2,1:T(8,128)(2,1)}), bf16[1024,4,192]{0,2,1:T(8,128)(2,1)S(1)}, u32[]{:S(2)}, u32[]{:S(2)}) async-start(bf16[1024,4,192]{0,2,1:T(8,128)(2,1)} %bitcast.68), calls=%async_computation.2 | async-start | bytes 3145728 | tf_op jit(solution)/shard_map/all_to_all | solution.py:208
  451.4 200.5 %reduce-scatter.12.cloned.1.call-start = ((), (), s32[]{:S(2)}) async-start(), calls=%async_computation.13 | async-start | bytes 7864320 | tf_op jit(solution)/shard_map/reduce_scatter | solution.py:233
  593.4 361.3 %reduce-scatter.16.cloned.1.call-start = ((), (), s32[]{:S(2)}) async-start(), calls=%async_computation.15 | async-start | bytes 2654208 | tf_op jit(solution)/shard_map/reduce_scatter | solution.py:273
  598.8 53.1 %copy-start.1 = (f32[1024,768]{0,1:T(8,128)S(1)}, f32[1024,768]{0,1:T(8,128)}, u32[]{:S(2)}) copy-start(f32[1024,768]{0,1:T(8,128)} %copy-done) | copy-start | bytes 9437188
  598.8 53.1 %copy-start.34 = (f32[1024]{0:T(1024)S(1)}, f32[1024]{0:T(1024)}, u32[]{:S(2)}) copy-start(f32[1024]{0:T(1024)} %copy-done.33) | copy-start | bytes 12292
  598.8 53.1 %copy-start.36 = (f32[768]{0:T(1024)S(1)}, f32[768]{0:T(1024)}, u32[]{:S(2)}) copy-start(f32[768]{0:T(1024)} %copy-done.35) | copy-start | bytes 9220
  598.8 53.1 %copy-start.38 = (f32[1024]{0:T(1024)S(1)}, f32[1024]{0:T(1024)}, u32[]{:S(2)}) copy-start(f32[1024]{0:T(1024)} %copy-done.37) | copy-start | bytes 12292
  693.2 385.8 %reduce-scatter.18.cloned.1.call-start = ((), (), s32[]{:S(2)}) async-start(), calls=%async_computation.16 | async-start | bytes 21233664 | tf_op jit(solution)/shard_map/reduce_scatter | solution.py:270
  763.2 24.5 %all-to-all-start.3 = ((bf16[1024,4,192]{0,2,1:T(8,128)(2,1)}), bf16[1024,4,192]{0,2,1:T(8,128)(2,1)}, u32[]{:S(2)}, u32[]{:S(2)}) async-start(bf16[1024,4,192]{0,2,1:T(8,128)(2,1)} %bitcast.483), calls=%async_computation.4 | async-start | bytes 3145728 | tf_op jit(solution)/shard_map/all_to_all | solution.py:208
  767.6 436.8 %all-reduce.3.cloned.1.call-start = ((), (), s32[]{:S(2)}) async-start(), calls=%async_computation.20 | async-start | bytes 147456 | tf_op jit(solution)/shard_map/psum | solution.py:288
  932.0 344.8 %reduce-scatter.22.cloned.1.call-start = ((), (), s32[]{:S(2)}) async-start(), calls=%async_computation.18 | async-start | bytes 1990656
  954.6 345.0 %reduce-scatter.24.cloned.1.call-start = ((), (), s32[]{:S(2)}) async-start(), calls=%async_computation.19 | async-start | bytes 491520
  957.0 403.6 %reduce-scatter.14.cloned.1.call-start = ((), (), s32[]{:S(2)}) async-start(), calls=%async_computation.14 | async-start | bytes 7864320 | tf_op jit(solution)/shard_map/reduce_scatter | solution.py:233
  966.8 429.4 %reduce-scatter.20.cloned.1.call-start = ((), (), s32[]{:S(2)}) async-start(), calls=%async_computation.17 | async-start | bytes 2949120 | tf_op jit(solution)/shard_map/reduce_scatter | solution.py:281
  (75 other events, 1029.3 us)
Sparse Core Ops, SparseCore 0:
  9.6 49.0 all-gather.2
  208.7 46.3 all-gather.4
  593.5 58.3 reduce-scatter.11
  693.3 69.0 reduce-scatter.15
  766.6 312.3 reduce-scatter.17
  1086.6 117.7 all-reduce.2
  1208.2 68.5 reduce-scatter.21
  1279.9 19.7 reduce-scatter.23
  1302.2 58.3 reduce-scatter.13
  1363.1 33.0 reduce-scatter.19
where the time goes:
time: 1420 us; the launch traced here: 1410 us
  waiting for transfers between devices  610 us (43%)
  matrix products  475 us (33%)
  local copies, waits for them, and re-layouts  185 us (13%)
  other arithmetic  102 us (7%)
  starting transfers between devices  17.2 us (1%)
  between operations  15.7 us (1%)
    psum x1, waiting for transfers between devices, on_device(): small_sum, shift_sum = lax.psum((small_stack, shift_stack), ('dp', 'head'))  123 us
    reduce_scatter x1, waiting for transfers between devices, on_device(): lax.psum_scatter(ffn_stack.astype(jnp.bfloat16), 'dp', scatter_dimension=...  112 us
    reduce_scatter x2, waiting for transfers between devices, on_device(): lax.psum_scatter(jnp.einsum('rce,cde->rd', grad_proj, layer_weights, pref...  101 us
    all_gather x2, waiting for transfers between devices, on_device(): lax.all_gather(hidden_state.astype(jnp.bfloat16), 'head', axis=0, tiled=T...  92.3 us
    unnamed x12, waiting for transfers between devices  89.2 us
    dot_general x2, matrix products, on_device(): jnp.dot(ffn_rows, up_part, preferred_element_type=jnp.float32) + up_shift  77.2 us
    unnamed x195, local copies, waits for them, and re-layouts  57.6 us
    dot_general x32, matrix products, slot_scores(): jnp.einsum('qhd,khd->hqk', queries, keys_in, preferred_element_type=jnp.f...  55.1 us
  transfers between devices with their start and end apart: 14, of which 13 were waited for; matrix products, arithmetic and copies ran while one was open for 21% of the time, Pallas kernels for 0%

commit v1 on v0

--- a/solution.py
+++ b/solution.py
@@ -5,6 +5,18 @@
 
 HD = 64
 EPSILON = 1e-06
+
+
+def gather_by_bits(array, axis, dim):
+    ways, here = (lax.axis_size(axis), lax.axis_index(axis))
+    grown, reach = (array, 1)
+    while reach < ways:
+        theirs = lax.ppermute(grown, axis, [(d, d ^ reach) for d in range(ways)])
+        mine_first = jnp.concatenate([grown, theirs], axis=dim)
+        theirs_first = jnp.concatenate([theirs, grown], axis=dim)
+        grown = jnp.where(here & reach == 0, mine_first, theirs_first)
+        reach = 2 * reach
+    return grown
 
 
 def norm_rows(values, gain, shift):
@@ -107,7 +119,7 @@
     hidden_state = tokens.astype(jnp.float32)
     kept_values = []
     for layer_index in range(layers):
-        gathered = lax.all_gather(hidden_state.astype(jnp.bfloat16), "head", axis=0, tiled=True)
+        gathered = gather_by_bits(hidden_state.astype(jnp.bfloat16), "head", 0)
         projected = jnp.einsum(
             "rd,cde->rce", gathered, qkv_weight[layer_index], preferred_element_type=jnp.float32
         )

time: 1420 us -> 1480 us (1.042)
  waiting for transfers between devices: 610 us -> 658 us
    ppermute x0 -> x4, waiting for transfers between devices: none -> 143 us  [gather_by_bits(): theirs = lax.ppermute(grown, axis, [(d, d ^ reach) for d in range(ways)])]
    all_gather x2 -> x0, waiting for transfers between devices: 92.3 us -> none  [on_device(): lax.all_gather(hidden_state.astype(jnp.bfloat16), 'head', axis=0, tiled=T...]
    unnamed x12 -> x10, waiting for transfers between devices: 89.2 us -> 88.3 us
    unnamed x195 -> x203, local copies, waits for them, and re-layouts: 57.6 us -> 57.9 us
  transfers between devices with their start and end apart: 14 -> 16, of which waited for: 13 -> 15; matrix products, arithmetic and copies ran while one was open for 21% -> 21% of each run, Pallas kernels for 0% -> 0%
where the time goes in v1:
time: 1480 us; the launch traced here: 1460 us
  waiting for transfers between devices  658 us (44%)
  matrix products  485 us (33%)
  local copies, waits for them, and re-layouts  173 us (12%)
  other arithmetic  107 us (7%)
  starting transfers between devices  20.4 us (1%)
  between operations  15.7 us (1%)
    ppermute x4, waiting for transfers between devices, gather_by_bits(): theirs = lax.ppermute(grown, axis, [(d, d ^ reach) for d in range(ways)])  143 us
    psum x1, waiting for transfers between devices, on_device(): small_sum, shift_sum = lax.psum((small_stack, shift_stack), ('dp', 'head'))  123 us
    reduce_scatter x1, waiting for transfers between devices, on_device(): lax.psum_scatter(ffn_stack.astype(jnp.bfloat16), 'dp', scatter_dimension=...  110 us
    reduce_scatter x2, waiting for transfers between devices, on_device(): lax.psum_scatter(jnp.einsum('rce,cde->rd', grad_proj, layer_weights, pref...  101 us
    unnamed x10, waiting for transfers between devices  88.3 us
    dot_general x2, matrix products, on_device(): jnp.dot(ffn_rows, up_part, preferred_element_type=jnp.float32) + up_shift  77.9 us
    unnamed x203, local copies, waits for them, and re-layouts  57.9 us
    dot_general x32, matrix products, slot_scores(): jnp.einsum('qhd,khd->hqk', queries, keys_in, preferred_element_type=jnp.f...  55.1 us
  transfers between devices with their start and end apart: 16, of which 15 were waited for; matrix products, arithmetic and copies ran while one was open for 21% of the time, Pallas kernels for 0%

profile of v1, /device:TPU:0, one launch (start us, length us, event | category | flops | bytes accessed | tf_op | source)
XLA Modules:
  0.0 1461.1 jit_solution(7953025597665729020)
XLA Ops:
  21.9 66.6 %collective-permute-done.1 = bf16[2048,768]{0,1:T(8,128)(2,1)} collective-permute-done((bf16[2048,768]{0,1:T(8,128)(2,1)}, bf16[2048,768]{0,1:T(8,128)(2,1)}, u32[]{:S(2)}, u32[]{:S(2)}) %collective-permute-start.1) | collective-permute-done | bytes 3145760 | tf_op jit(solution)/shard_map/ppermute | solution.py:14
  106.6 35.6 %while.52 = (s32[]{:T(128)}, bf16[8,512,3,64]{1,3,2,0:T(8,128)(2,1)}, f32[8,3,512]{2,1,0:T(4,128)S(1)}, bf16[8,512,3,64]{1,3,2,0:T(8,128)(2,1)}, s32[8,512]{1,0:...) while((s32[]{:T(128)}, ...), condition=%wide.region_5.6_spmd, body=%wide.region_2.5_spmd.sunk | while | flops 211122688 | bytes 11335773 | solution.py:135
  160.4 16.9 %all-to-all-done = bf16[4,1024,192]{1,2,0:T(8,128)(2,1)S(1)} async-done(((bf16[4,1024,192]{1,2,0:T(8,128)(2,1)}), bf16[4,1024,192]{1,2,0:T(8,128)(2,1)S(1)}, u32[]{:S(2)}, u32[]{:S(2)}) %all-to-all-start) | async-done | bytes 1572896 | tf_op jit(solution)/shard_map/all_to_all | solution.py:139
  181.4 39.3 %multiply_convert_fusion.3 = (bf16[1024,3072]{1,0:T(8,128)(2,1)}, f32[1024,3072]{1,0:T(8,128)}, f32[1024,3072]{1,0:T(8,128)}) fusion(f32[3072]{0:T(1024)S(1)} %bitcast.492, bf16[2,768,3072]{2,1,0:T(8,128)(2,1)} %param.31, f32[1024,768]{0,1:T(8,128)S(1)} %get-tuple-element.478, f32[768]{0:T(1024)S(1)} %get-tuple-element.347, ...), kind=kOutput, calls=%fused_computation.148 | convolution fusion | flops 5043388416 | bytes 39348224 | tf_op jit(solution)/shard_map/dot_general | solution.py:151
  236.5 70.1 %collective-permute-done.3 = bf16[2048,768]{0,1:T(8,128)(2,1)} collective-permute-done((bf16[2048,768]{0,1:T(8,128)(2,1)}, bf16[2048,768]{0,1:T(8,128)(2,1)}, u32[]{:S(2)}, u32[]{:S(2)}) %collective-permute-start.3) | collective-permute-done | bytes 3145760 | tf_op jit(solution)/shard_map/ppermute | solution.py:14
  327.2 43.5 %while.53 = (s32[]{:T(128)}, bf16[8,512,3,64]{1,3,2,0:T(8,128)(2,1)}, f32[8,3,512]{2,1,0:T(4,128)S(1)}, bf16[8,512,3,64]{1,3,2,0:T(8,128)(2,1)}, s32[8,512]{1,0:...) while((s32[]{:T(128)}, ...), condition=%wide.region_13.14_spmd, body=%wide.region_10.13_spmd.sunk | while | flops 211122688 | bytes 11335773 | solution.py:135
  388.4 17.5 %all-to-all-done.1 = bf16[4,1024,192]{1,2,0:T(8,128)(2,1)} async-done(((bf16[4,1024,192]{1,2,0:T(8,128)(2,1)}), bf16[4,1024,192]{1,2,0:T(8,128)(2,1)}, u32[]{:S(2)}, u32[]{:S(2)}) %all-to-all-start.1) | async-done | bytes 1572896 | tf_op jit(solution)/shard_map/all_to_all | solution.py:139
  410.6 38.6 %multiply_convert_fusion.2 = (bf16[1024,3072]{1,0:T(8,128)(2,1)}, f32[1024,3072]{1,0:T(8,128)}, f32[1024,3072]{1,0:T(8,128)}) fusion(f32[3072]{0:T(1024)S(1)} %bitcast.495, bf16[2,768,3072]{2,1,0:T(8,128)(2,1)} %param.31, f32[1024,768]{0,1:T(8,128)S(1)} %get-tuple-element.483, f32[768]{0:T(1024)S(1)} %copy-done.75, f32[768]{0:T(1024)S(1)} %copy-done.54, ...), kind=kOutput, calls=%fused_computation.135 | convolution fusion | flops 5043388416 | bytes 39348224 | tf_op jit(solution)/shard_map/dot_general | solution.py:151
  465.5 18.1 %convert_reduce_fusion = (f32[3072]{0:T(1024)}, bf16[1024,3072]{1,0:T(8,128)(2,1)}) fusion(f32[1024,3072]{1,0:T(8,128)} %get-tuple-element.435, bf16[1024,768]{0,1:T(8,128)(2,1)S(1)} %get-tuple-element.425, bf16[2,3072,768]{2,1,0:T(8,128)(2,1)} %param.33, f32[1024,3072]{1,0:T(8,128)} %get-tuple-element.484, f32[3072]{0:T(1024)S(1)} %bitcast.496), kind=kOutput, calls=%fused_computation.131 | convolution fusion | flops 4885312512 | bytes 37773312 | tf_op jit(solution)/shard_map/rd,fd->rf/dot_general | solution.py:197
  483.6 11.7 multiply_reduce_fusion.2
  505.7 20.0 %all-to-all-done.2 = bf16[1024,4,192]{0,2,1:T(8,128)(2,1)S(1)} async-done(((bf16[1024,4,192]{0,2,1:T(8,128)(2,1)}), bf16[1024,4,192]{0,2,1:T(8,128)(2,1)S(1)}, u32[]{:S(2)}, u32[]{:S(2)}) %all-to-all-start.2) | async-done | bytes 1572896 | tf_op jit(solution)/shard_map/all_to_all | solution.py:220
  533.8 88.1 %while.54 = (s32[]{:T(128)}, bf16[8,512,3,64]{1,3,2,0:T(8,128)(2,1)S(1)}, bf16[8,512,3,64]{1,3,2,0:T(8,128)(2,1)}, bf16[8,512,3,64]{1,3,2,0:T(8,128)(2,1)}, bf16...) while((s32[]{:T(128)}, ...), condition=%wide.region_24.25_spmd, body=%wide.region_22.24_spmd.sunk | while | flops 511146496 | bytes 26125428 | solution.py:222
  653.1 12.0 fusion.140
  665.1 41.6 %reduce-scatter.12.cloned.1.call-done = bf16[1024,768]{0,1:T(8,128)(2,1)} async-done(((bf16[4096,768]{0,1:T(8,128)(2,1)}), bf16[1024,768]{0,1:T(8,128)(2,1)}) %reduce-scatter.12.cloned.1.call-update) | async-done | bytes 1572880 | tf_op jit(solution)/shard_map/reduce_scatter | solution.py:245
  714.1 18.5 %convert_reduce_fusion.1 = (f32[3072]{0:T(1024)S(1)}, bf16[1024,3072]{1,0:T(8,128)(2,1)}) fusion(f32[1024,3072]{1,0:T(8,128)} %get-tuple-element.437, bf16[1024,768]{0,1:T(8,128)(2,1)} %get-tuple-element.421, bf16[2,3072,768]{2,1,0:T(8,128)(2,1)} %param.33, f32[1024,3072]{1,0:T(8,128)} %get-tuple-element.479, f32[3072]{0:T(1024)S(1)} %bitcast.493), kind=kOutput, calls=%fused_computation.132 | convolution fusion | flops 4885312512 | bytes 37773312 | tf_op jit(solution)/shard_map/rd,fd->rf/dot_general | solution.py:197
  793.0 16.7 %pad_maximum_fusion = bf16[2,2,768,3072]{3,2,1,0:T(8,128)(2,1)} fusion(bf16[1,2,768,3072]{3,2,1,0:T(8,128)(2,1)} %maximum_bitcast_fusion.1, bf16[1,2,768,3072]{3,2,1,0:T(8,128)(2,1)} %maximum_bitcast_fusion), kind=kLoop, calls=%fused_computation.126 | loop fusion | flops 9437184 | bytes 37748736 | tf_op jit(solution)/shard_map/stack | solution.py:276
  822.6 11.2 fusion.173
  857.2 101.9 %while.55 = (s32[]{:T(128)}, bf16[8,512,3,64]{1,3,2,0:T(8,128)(2,1)}, bf16[8,512,3,64]{1,3,2,0:T(8,128)(2,1)}, bf16[8,512,3,64]{1,3,2,0:T(8,128)(2,1)}, bf16[8,5...) while((s32[]{:T(128)}, ...), condition=%wide.region_32.33_spmd, body=%wide.region_30.32_spmd.sunk | while | flops 511146496 | bytes 26125428 | solution.py:222
  1023.9 110.1 %reduce-scatter.18.cloned.1.call-done = bf16[2,2,96,3072]{3,2,1,0:T(8,128)(2,1)} async-done(((bf16[2,2,768,3072]{3,2,1,0:T(8,128)(2,1)}), bf16[2,2,96,3072]{3,2,1,0:T(8,128)(2,1)}) %reduce-scatter.18.cloned.1.call-update) | async-done | bytes 2359312 | tf_op jit(solution)/shard_map/reduce_scatter | solution.py:282
  1136.6 122.8 %all-reduce.3.cloned.1.call-done = (f32[2,8,768]{2,0,1:T(2,128)}, f32[2,3072]{1,0:T(2,128)}) async-done(((f32[2,8,768]{2,0,1:T(2,128)}, f32[2,3072]{1,0:T(2,128)}), (f32[2,8,768]{2,0,1:T(2,128)}, f32[2,3072]{1,0:T(2,128)})) %all-reduce.3.cloned.1.call-update) | async-done | bytes 73744 | tf_op jit(solution)/shard_map/psum | solution.py:300
  1262.1 69.7 %reduce-scatter.22.cloned.1.call-done = bf16[96,1152]{1,0:T(8,128)(2,1)} async-done(((bf16[768,1152]{1,0:T(8,128)(2,1)}), bf16[96,1152]{1,0:T(8,128)(2,1)}) %reduce-scatter.22.cloned.1.call-update) | async-done | bytes 221200
  1336.1 18.4 %reduce-scatter.24.cloned.1.call-done = bf16[192,192]{1,0:T(8,128)(2,1)} async-done(((bf16[768,192]{1,0:T(8,128)(2,1)}), bf16[192,192]{1,0:T(8,128)(2,1)}) %reduce-scatter.24.cloned.1.call-update) | async-done | bytes 73744
  1356.3 59.1 %reduce-scatter.14.cloned.1.call-done = bf16[1024,768]{0,1:T(8,128)(2,1)} async-done(((bf16[4096,768]{0,1:T(8,128)(2,1)}), bf16[1024,768]{0,1:T(8,128)(2,1)}) %reduce-scatter.14.cloned.1.call-update) | async-done | bytes 1572880 | tf_op jit(solution)/shard_map/reduce_scatter | solution.py:245
  1421.2 30.1 %reduce-scatter.20.cloned.1.call-done = bf16[2,2,96,768]{3,2,1,0:T(8,128)(2,1)} async-done(((bf16[2,2,96,3072]{3,2,1,0:T(8,128)(2,1)}), bf16[2,2,96,768]{3,2,1,0:T(8,128)(2,1)}) %reduce-scatter.20.cloned.1.call-update) | async-done | bytes 589840 | tf_op jit(solution)/shard_map/reduce_scatter | solution.py:293
  (611 shorter events, 635.2 us)
Async XLA Ops:
  8.9 3.7 collective-permute-start
  16.9 71.6 %collective-permute-start.1 = (bf16[2048,768]{0,1:T(8,128)(2,1)}, bf16[2048,768]{0,1:T(8,128)(2,1)}, u32[]{:S(2)}, u32[]{:S(2)}) collective-permute-start(bf16[2048,768]{0,1:T(8,128)(2,1)} %maximum_select_fusion.2), channel_id=1, source_target_pairs={{0,2},{1,3},{2,0},{3,1},{4,6},{5,7},{6,4},{7,5},{8,10},{9,11},{10,... | collective-permute-start | bytes 9437192 | tf_op jit(solution)/shard_map/ppermute | solution.py:14
  153.6 23.7 %all-to-all-start = ((bf16[4,1024,192]{1,2,0:T(8,128)(2,1)}), bf16[4,1024,192]{1,2,0:T(8,128)(2,1)S(1)}, u32[]{:S(2)}, u32[]{:S(2)}) async-start(bf16[4,1024,192]{1,2,0:T(8,128)(2,1)} %copy.179), calls=%async_computation | async-start | bytes 3145728 | tf_op jit(solution)/shard_map/all_to_all | solution.py:139
  159.2 61.5 %copy-start.52 = (f32[768]{0:T(1024)}, f32[768]{0:T(1024)S(1)}, u32[]{:S(2)}) copy-start(f32[768]{0:T(1024)S(1)} %get-tuple-element.495) | copy-start | bytes 9220
  159.2 61.6 %copy-start.73 = (f32[768]{0:T(1024)}, f32[768]{0:T(1024)S(1)}, u32[]{:S(2)}) copy-start(f32[768]{0:T(1024)S(1)} %get-tuple-element.347) | copy-start | bytes 9220
  159.8 246.1 %copy-start.37 = (f32[768]{0:T(1024)}, f32[768]{0:T(1024)S(1)}, u32[]{:S(2)}) copy-start(f32[768]{0:T(1024)S(1)} %get-tuple-element.497) | copy-start | bytes 9220
  229.4 176.5 %copy-start = (f32[1024,768]{0,1:T(8,128)}, f32[1024,768]{0,1:T(8,128)S(1)}, u32[]{:S(2)}) copy-start(f32[1024,768]{0,1:T(8,128)S(1)} %get-tuple-element.481) | copy-start | bytes 9437188
  229.4 176.5 %copy-start.35 = (f32[1024]{0:T(1024)}, f32[1024]{0:T(1024)S(1)}, u32[]{:S(2)}) copy-start(f32[1024]{0:T(1024)S(1)} %broadcast_multiply_fusion.2) | copy-start | bytes 12292
  229.9 176.1 %copy-start.39 = (f32[1024]{0:T(1024)}, f32[1024]{0:T(1024)S(1)}, u32[]{:S(2)}) copy-start(f32[1024]{0:T(1024)S(1)} %fusion.192) | copy-start | bytes 12292
  230.4 3.5 collective-permute-start.2
  236.2 70.5 %collective-permute-start.3 = (bf16[2048,768]{0,1:T(8,128)(2,1)}, bf16[2048,768]{0,1:T(8,128)(2,1)}, u32[]{:S(2)}, u32[]{:S(2)}) collective-permute-start(bf16[2048,768]{0,1:T(8,128)(2,1)} %maximum_select_fusion.3), channel_id=1, source_target_pairs={{0,2},{1,3},{2,0},{3,1},{4,6},{5,7},{6,4},{7,5},{8,10},{9,11},{10,... | collective-permute-start | bytes 9437192 | tf_op jit(solution)/shard_map/ppermute | solution.py:14
  381.1 24.8 %all-to-all-start.1 = ((bf16[4,1024,192]{1,2,0:T(8,128)(2,1)}), bf16[4,1024,192]{1,2,0:T(8,128)(2,1)}, u32[]{:S(2)}, u32[]{:S(2)}) async-start(bf16[4,1024,192]{1,2,0:T(8,128)(2,1)} %copy.185), calls=%async_computation.1 | async-start | bytes 3145728 | tf_op jit(solution)/shard_map/all_to_all | solution.py:139
  502.1 23.6 %all-to-all-start.2 = ((bf16[1024,4,192]{0,2,1:T(8,128)(2,1)}), bf16[1024,4,192]{0,2,1:T(8,128)(2,1)S(1)}, u32[]{:S(2)}, u32[]{:S(2)}) async-start(bf16[1024,4,192]{0,2,1:T(8,128)(2,1)} %bitcast.68), calls=%async_computation.2 | async-start | bytes 3145728 | tf_op jit(solution)/shard_map/all_to_all | solution.py:220
  505.7 201.1 %reduce-scatter.12.cloned.1.call-start = ((), (), s32[]{:S(2)}) async-start(), calls=%async_computation.11 | async-start | bytes 7864320 | tf_op jit(solution)/shard_map/reduce_scatter | solution.py:245
  647.7 364.3 %reduce-scatter.16.cloned.1.call-start = ((), (), s32[]{:S(2)}) async-start(), calls=%async_computation.13 | async-start | bytes 2654208 | tf_op jit(solution)/shard_map/reduce_scatter | solution.py:285
  653.1 53.6 %copy-start.36 = (f32[1024]{0:T(1024)S(1)}, f32[1024]{0:T(1024)}, u32[]{:S(2)}) copy-start(f32[1024]{0:T(1024)} %copy-done.35) | copy-start | bytes 12292
  653.1 53.6 %copy-start.38 = (f32[768]{0:T(1024)S(1)}, f32[768]{0:T(1024)}, u32[]{:S(2)}) copy-start(f32[768]{0:T(1024)} %copy-done.37) | copy-start | bytes 9220
  748.2 385.9 %reduce-scatter.18.cloned.1.call-start = ((), (), s32[]{:S(2)}) async-start(), calls=%async_computation.14 | async-start | bytes 21233664 | tf_op jit(solution)/shard_map/reduce_scatter | solution.py:282
  818.2 24.5 %all-to-all-start.3 = ((bf16[1024,4,192]{0,2,1:T(8,128)(2,1)}), bf16[1024,4,192]{0,2,1:T(8,128)(2,1)}, u32[]{:S(2)}, u32[]{:S(2)}) async-start(bf16[1024,4,192]{0,2,1:T(8,128)(2,1)} %bitcast.481), calls=%async_computation.4 | async-start | bytes 3145728 | tf_op jit(solution)/shard_map/all_to_all | solution.py:220
  822.6 436.9 %all-reduce.3.cloned.1.call-start = ((), (), s32[]{:S(2)}) async-start(), calls=%async_computation.18 | async-start | bytes 147456 | tf_op jit(solution)/shard_map/psum | solution.py:300
  987.2 344.7 %reduce-scatter.22.cloned.1.call-start = ((), (), s32[]{:S(2)}) async-start(), calls=%async_computation.16 | async-start | bytes 1990656
  1011.9 342.6 %reduce-scatter.24.cloned.1.call-start = ((), (), s32[]{:S(2)}) async-start(), calls=%async_computation.17 | async-start | bytes 491520
  1014.3 401.2 %reduce-scatter.14.cloned.1.call-start = ((), (), s32[]{:S(2)}) async-start(), calls=%async_computation.12 | async-start | bytes 7864320 | tf_op jit(solution)/shard_map/reduce_scatter | solution.py:245
  1023.9 427.4 %reduce-scatter.20.cloned.1.call-start = ((), (), s32[]{:S(2)}) async-start(), calls=%async_computation.15 | async-start | bytes 2949120 | tf_op jit(solution)/shard_map/reduce_scatter | solution.py:293
  (81 other events, 1193.7 us)
Sparse Core Ops, SparseCore 0:
  647.8 58.9 reduce-scatter.11
  748.3 68.9 reduce-scatter.15
  821.7 312.3 reduce-scatter.17
  1141.6 117.7 all-reduce.2
  1263.1 68.6 reduce-scatter.21
  1334.8 19.7 reduce-scatter.23
  1357.1 58.3 reduce-scatter.13
  1418.2 33.0 reduce-scatter.19
